TPU v7x, 256 devices: a whole 4x4x8 slice. The times are simulated.
256 devices in a mesh: shift: 4 (over x), fsdp: 32 (over z, y_lo, core), tp: 2 (over y_hi).
Axes of the slice: x: 4, y: 4 (y_hi: 2, y_lo: 2; y = y_hi * 2 + y_lo), z: 8, core: 2. Of those that a mesh axis runs over, the one named last changes fastest.
Arguments:
- grad_stack: float32 [512, 128, 2048], P('shift', 'fsdp', 'tp'), parts along dimension 0, may hold values from -6 to 6
- moment_stack: float32 [512, 128, 2048], P('shift', 'fsdp', 'tp'), parts along dimension 0, may hold values from -6 to 6
- weight_stack: float32 [512, 128, 2048], P('shift', 'fsdp', 'tp'), parts along dimension 0, may hold values from -0.1875 to 0.1875
Outputs:
- new_weights: float32 [512, 128, 2048], P('shift', 'fsdp', 'tp'), parts along dimension 0
- new_momentum: float32 [512, 128, 2048], P('shift', 'fsdp', 'tp'), parts along dimension 0
There are 4 independent parts, one for each index of `shift`. A program takes and returns all parts, laid end to end along the dimension named above; each array names one. Nothing has to cross between parts.
All inputs are finite; a program needn't handle non-finite values.
Results may differ from a plain program's by a relative error of at most 0.0003.
Values sent between devices are 32-bit elements.
A program may use at most 64 MiB of HBM per device.

v0:
```python
import jax
import jax.numpy as jnp
from jax import lax
from jax.sharding import PartitionSpec as P

ITERS = 3


hold_rate = 0.95
learn_rate = 0.9


def gathered_total(array, axis):
    return lax.all_gather(array, axis).sum(0)


def body(grad_stack, moment_stack, weight_stack):
    new_momentum = hold_rate * moment_stack + grad_stack
    moved = lax.all_to_all(new_momentum, "fsdp", split_axis=0, concat_axis=1, tiled=True)
    total = gathered_total(jnp.sum(moved * moved, axis=(1, 2), keepdims=True), "tp")
    iterate = moved * lax.rsqrt(total + 1e-06)
    for step in range(ITERS):
        gram = gathered_total(
            jnp.einsum("mik,mjk->mij", iterate, iterate, precision=lax.Precision.HIGHEST), "tp"
        )
        mixed = -4.775 * gram + 2.0315 * jnp.einsum(
            "mij,mjk->mik", gram, gram, precision=lax.Precision.HIGHEST
        )
        iterate = 3.4445 * iterate + jnp.einsum(
            "mij,mjk->mik", mixed, iterate, precision=lax.Precision.HIGHEST
        )
    back = lax.all_to_all(iterate, "fsdp", split_axis=1, concat_axis=0, tiled=True)
    new_weights = weight_stack - learn_rate * back
    return (new_weights, new_momentum)


def solution(mesh):
    in_specs = (P("shift", "fsdp", "tp"), P("shift", "fsdp", "tp"), P("shift", "fsdp", "tp"))
    out_specs = (P("shift", "fsdp", "tp"), P("shift", "fsdp", "tp"))
    return jax.shard_map(body, mesh=mesh, in_specs=in_specs, out_specs=out_specs, check_vma=False)
```

profile of v0, /device:TPU:1, one launch (start us, length us, event | category | flops | bytes accessed | tf_op | source)
XLA Modules:
  0.0 186.9 jit_solution(4581866831942809648)
XLA Ops:
  0.6 4.6 %multiply_add_fusion.3 = f32[128,4,1024]{2,1,0:T(4,128)} fusion(f32[128,4,1024]{2,1,0:T(4,128)} %param.3, f32[128,4,1024]{2,1,0:T(4,128)} %param.4), kind=kLoop, calls=%fused_computation.6 | loop fusion | flops 1048576 | bytes 6291456 | tf_op jit(solution)/shard_map/add | solution.py:18
  5.2 11.3 %all-to-all-start = ((f32[128,4,1024]{2,1,0:T(4,128)}), f32[128,4,1024]{2,1,0:T(4,128)S(1)}, u32[]{:S(2)}, u32[]{:S(2)}) async-start(f32[128,4,1024]{2,1,0:T(4,128)} %multiply_add_fusion.3), calls=%async_computation | async-start | bytes 4194304 | tf_op jit(solution)/shard_map/all_to_all | solution.py:19
  16.5 0.6 dynamic-slice
  17.7 48.8 %all-to-all-done = f32[128,4,1024]{2,1,0:T(4,128)S(1)} async-done(((f32[128,4,1024]{2,1,0:T(4,128)}), f32[128,4,1024]{2,1,0:T(4,128)S(1)}, u32[]{:S(2)}, u32[]{:S(2)}) %all-to-all-start) | async-done | bytes 2097184 | tf_op jit(solution)/shard_map/all_to_all | solution.py:19
  66.5 0.6 multiply_reduce_fusion
  67.4 5.3 %all-reduce = f32[8]{0:T(128)S(1)} all-reduce(f32[8]{0:T(128)S(1)} %dynamic-update-slice), channel_id=2, replica_groups=mesh['shift'=4,'fsdp'=32,'tp'=2] {'tp'}, use_global_device_ids=true, to_apply=%add | all-reduce | flops 8 | bytes 64
  72.7 1.5 copy_bitcast_fusion
  74.3 2.0 %all_to_all.23 = f32[4,128,1024]{2,1,0:T(8,128)S(1)} reshape(f32[4,32,4,1024]{3,2,1,0:T(4,128)} %copy_bitcast_fusion) | data formatting | bytes 4194304 | tf_op jit(solution)/shard_map/all_to_all | solution.py:19
  76.3 2.3 %fusion.2 = f32[4,128,128]{2,1,0:T(8,128)S(1)} fusion(f32[4,128,1024]{2,1,0:T(8,128)S(1)} %all_to_all.23, f32[4]{0:T(128)S(1)} %add_rsqrt_fusion), kind=kOutput, calls=%fused_computation.9 | convolution fusion | flops 805830656 | bytes 2359312 | tf_op jit(solution)/shard_map/mik,mjk->mij/dot_general | solution.py:24
  78.5 7.4 %all-gather.1 = f32[8,128,128]{2,1,0:T(8,128)S(1)} all-gather(f32[4,128,128]{2,1,0:T(8,128)S(1)} %fusion.2), channel_id=3, replica_groups=mesh['shift'=4,'fsdp'=32,'tp'=2] {'tp'}, dimensions={0}, use_global_device_ids=true | all-gather | bytes 786432 | tf_op jit(solution)/shard_map/all_gather | solution.py:14
  86.0 0.4 fusion.8
  86.4 4.3 %multiply_add_fusion.2 = f32[4,128,1024]{2,1,0:T(8,128)S(1)} fusion(f32[4,128,1024]{2,1,0:T(8,128)} %copy-done.1, f32[4,128,128]{2,1,0:T(8,128)S(1)} %fusion.8, f32[4]{0:T(128)S(1)} %add_rsqrt_fusion), kind=kOutput, calls=%fused_computation.4 | convolution fusion | flops 807403520 | bytes 4456464 | tf_op jit(solution)/shard_map/mij,mjk->mik/dot_general | solution.py:29
  90.7 2.0 %fusion.11 = f32[4,128,128]{2,1,0:T(8,128)S(1)} fusion(f32[4,128,1024]{2,1,0:T(8,128)S(1)} %multiply_add_fusion.2), kind=kOutput, calls=%fused_computation.21 | convolution fusion | flops 805306368 | bytes 2359296 | tf_op jit(solution)/shard_map/mik,mjk->mij/dot_general | solution.py:24
  92.7 7.6 %all-gather.2 = f32[8,128,128]{2,1,0:T(8,128)S(1)} all-gather(f32[4,128,128]{2,1,0:T(8,128)S(1)} %fusion.11), channel_id=4, replica_groups=mesh['shift'=4,'fsdp'=32,'tp'=2] {'tp'}, dimensions={0}, use_global_device_ids=true | all-gather | bytes 786432 | tf_op jit(solution)/shard_map/all_gather | solution.py:14
  100.3 0.4 fusion.7
  100.7 2.0 %multiply_add_fusion.1 = f32[4,128,1024]{2,1,0:T(8,128)S(1)} fusion(f32[4,128,1024]{2,1,0:T(8,128)S(1)} %multiply_add_fusion.2, f32[4,128,128]{2,1,0:T(8,128)S(1)} %fusion.7), kind=kOutput, calls=%fused_computation.3 | convolution fusion | flops 806354944 | bytes 4456448 | tf_op jit(solution)/shard_map/mij,mjk->mik/dot_general | solution.py:29
  102.8 2.0 %fusion.12 = f32[4,128,128]{2,1,0:T(8,128)S(1)} fusion(f32[4,128,1024]{2,1,0:T(8,128)S(1)} %multiply_add_fusion.1), kind=kOutput, calls=%fused_computation.22 | convolution fusion | flops 805306368 | bytes 2359296 | tf_op jit(solution)/shard_map/mik,mjk->mij/dot_general | solution.py:24
  104.8 7.4 %all-gather.3 = f32[8,128,128]{2,1,0:T(8,128)S(1)} all-gather(f32[4,128,128]{2,1,0:T(8,128)S(1)} %fusion.12), channel_id=5, replica_groups=mesh['shift'=4,'fsdp'=32,'tp'=2] {'tp'}, dimensions={0}, use_global_device_ids=true | all-gather | bytes 786432 | tf_op jit(solution)/shard_map/all_gather | solution.py:14
  112.6 4.2 %multiply_add_fusion = f32[4,128,1024]{2,1,0:T(8,128)S(1)} fusion(f32[4,128,1024]{2,1,0:T(8,128)} %copy-done, f32[4,128,128]{2,1,0:T(8,128)S(1)} %fusion.6), kind=kOutput, calls=%fused_computation.2 | convolution fusion | flops 806354944 | bytes 4456448 | tf_op jit(solution)/shard_map/mij,mjk->mik/dot_general | solution.py:29
  116.9 1.4 copy.8
  118.2 63.8 %all_to_all.27 = f32[4,128,1024]{2,0,1:T(4,128)S(1)} all-to-all(f32[4,128,1024]{2,0,1:T(4,128)S(1)} %copy.8), channel_id=1, replica_groups=mesh['shift'=4,'fsdp'=32,'tp'=2] {'fsdp'}, dimensions={1} | all-to-all | bytes 4194304 | tf_op jit(solution)/shard_map/all_to_all | solution.py:32
  182.0 0.7 broadcast_multiply_fusion
  182.7 1.8 copy.9
  184.5 2.4 %bitcast_subtract_fusion = f32[128,4,1024]{2,1,0:T(4,128)} fusion(f32[128,4,1024]{2,1,0:T(4,128)S(1)} %copy-done.2, f32[32,4,4,1024]{3,2,1,0:T(4,128)S(1)} %copy.9), kind=kLoop, calls=%fused_computation | loop fusion | flops 524288 | bytes 6291456 | tf_op jit(solution)/shard_map/sub | solution.py:33
  (17 shorter events, 0.8 us)
Async XLA Ops:
  5.2 11.3 %copy-start.3 = (u32[256]{0:T(256)S(1)}, u32[256]{0:T(256)}, u32[]{:S(2)}) copy-start(u32[256]{0:T(256)} %constant.19) | copy-start | bytes 3076
  5.2 61.3 %all-to-all-start = ((f32[128,4,1024]{2,1,0:T(4,128)}), f32[128,4,1024]{2,1,0:T(4,128)S(1)}, u32[]{:S(2)}, u32[]{:S(2)}) async-start(f32[128,4,1024]{2,1,0:T(4,128)} %multiply_add_fusion.3), calls=%async_computation | async-start | bytes 4194304 | tf_op jit(solution)/shard_map/all_to_all | solution.py:19
  76.3 9.7 %copy-start.1 = (f32[4,128,1024]{2,1,0:T(8,128)}, f32[4,128,1024]{2,1,0:T(8,128)S(1)}, u32[]{:S(2)}) copy-start(f32[4,128,1024]{2,1,0:T(8,128)S(1)} %all_to_all.23) | copy-start | bytes 6291460
  102.7 2.1 %copy-start = (f32[4,128,1024]{2,1,0:T(8,128)}, f32[4,128,1024]{2,1,0:T(8,128)S(1)}, u32[]{:S(2)}) copy-start(f32[4,128,1024]{2,1,0:T(8,128)S(1)} %multiply_add_fusion.1) | copy-start | bytes 6291460
  182.7 1.8 copy-start.2
where the time goes:
time: 187 us
  blocking collectives  91.4 us (49%)
  waiting for transfers between devices  48.8 us (26%)
  matrix products  18 us (10%)
  starting transfers between devices  11.3 us (6%)
  other arithmetic  8.38 us (4%)
  local copies, waits for them, and re-layouts  7.56 us (4%)
    all_to_all x1, blocking collectives, body(): lax.all_to_all(iterate, 'fsdp', split_axis=1, concat_axis=0, tiled=True)  63.8 us
    all_to_all x1, waiting for transfers between devices, body(): lax.all_to_all(new_momentum, 'fsdp', split_axis=0, concat_axis=1, tiled=T...  48.8 us
    all_gather x3, blocking collectives, gathered_total(): return lax.all_gather(array, axis).sum(0)  22.4 us
    all_to_all x1, starting transfers between devices, body(): lax.all_to_all(new_momentum, 'fsdp', split_axis=0, concat_axis=1, tiled=T...  11.3 us
    dot_general x3, matrix products, body(): jnp.einsum('mij,mjk->mik', mixed, iterate, precision=lax.Precision.HIGHEST)  10.6 us
    dot_general x3, matrix products, body(): jnp.einsum('mik,mjk->mij', iterate, iterate, precision=lax.Precision.HIGH...  6.35 us
    unnamed x1, blocking collectives  5.26 us
    add x1, other arithmetic, body(): new_momentum = hold_rate * moment_stack + grad_stack  4.57 us
  transfers between devices with their start and end apart: 1, of which 1 were waited for; matrix products, arithmetic and copies ran while one was open for 0% of the time, Pallas kernels for 0%

commit v1 on v0

v1 whole, which is shorter than its diff:
```python
import functools

import jax
import jax.numpy as jnp
from jax import lax
from jax.experimental import pallas as pl
from jax.experimental.pallas import tpu as pltpu
from jax.sharding import PartitionSpec as P

ITERS = 3
hold_rate = 0.95
learn_rate = 0.9

MESH = pl.DeviceIdType.MESH
HIGHEST = lax.Precision.HIGHEST
F32 = jnp.float32


def mul(a, b):
    return lax.dot_general(a, b, (((1,), (0,)), ((), ())), precision=HIGHEST, preferred_element_type=F32)


def mul_t(a, b):
    return lax.dot_general(a, b, (((1,), (1,)), ((), ())), precision=HIGHEST, preferred_element_type=F32)


def swap_rows(a, b):
    low = lax.broadcasted_iota(jnp.int32, a.shape, a.ndim - 2) < 4
    return (
        jnp.where(low, a, pltpu.roll(b, 4, a.ndim - 2)),
        jnp.where(low, pltpu.roll(a, 4, a.ndim - 2), b),
    )


def polynomial(gram):
    side = gram.shape[0]
    eye = (
        lax.broadcasted_iota(jnp.int32, gram.shape, 0) == lax.broadcasted_iota(jnp.int32, gram.shape, 1)
    ).astype(F32)
    total = jnp.sum(jnp.sum(gram * eye, axis=1, keepdims=True), axis=0, keepdims=True)
    scale = lax.rsqrt(total + 1e-06)
    gram = (gram * scale) * scale
    factor = None
    for step in range(ITERS):
        now = 3.4445 * eye - 4.775 * gram + 2.0315 * mul(gram, gram)
        if step < ITERS - 1:
            gram = mul(mul(now, gram), now)
        factor = now if factor is None else mul(now, factor)
    return factor * scale


def kernel(n, chunks, grad_hbm, moment_hbm, back, mom, grads, moments, taken, made, wide, gram_own, gram_other,
           load_sem, send_sem, in_sem, gram_send_sem, gram_sem, back_sem):
    me = lax.axis_index("fsdp")
    tp = lax.axis_index("tp")
    peer = 1 - tp

    def loads(m):
        rows = pl.ds(m * n, n)
        return (
            pltpu.make_async_copy(grad_hbm.at[rows], grads.at[rows], load_sem.at[0, m]),
            pltpu.make_async_copy(moment_hbm.at[rows], moments.at[rows], load_sem.at[1, m]),
        )

    for m in range(chunks):
        for copy in loads(m):
            copy.start()

    barrier = pltpu.get_barrier_semaphore()

    def greet(k, carry):
        pl.semaphore_signal(barrier, inc=1, device_id={"fsdp": lax.rem(me + k, n)}, device_id_type=MESH)
        return carry

    lax.fori_loop(1, n, greet, 0)
    pl.semaphore_signal(barrier, inc=1, device_id={"tp": peer}, device_id_type=MESH)

    def momentum(m):
        for copy in loads(m):
            copy.wait()
        rows = pl.ds(m * n, n)
        mom[rows] = hold_rate * moments[rows] + grads[rows]
        taken[m * n + me] = mom[m * n + me]

    momentum(0)
    pl.semaphore_wait(barrier, n)

    def scatter(m):
        def send(to):
            pltpu.make_async_remote_copy(
                src_ref=mom.at[m * n + to], dst_ref=taken.at[m * n + me], send_sem=send_sem, recv_sem=in_sem.at[m],
                device_id={"fsdp": to}, device_id_type=MESH).start()

        def pair(k, carry):
            send(lax.rem(me + n // 2 - k, n))
            send(lax.rem(me + n // 2 + k, n))
            return carry

        send(lax.rem(me + n // 2, n))
        lax.fori_loop(1, n // 2, pair, 0)

    for m in range(chunks):
        if m:
            momentum(m)
        scatter(m)

    def wait_for(buffer, sem, m):
        part = buffer.at[pl.ds(m * n, n - 1)]
        pltpu.make_async_copy(part, part, sem).wait()

    def compute(m, carry):
        wait_for(taken, in_sem.at[m], m)
        for j in range(4):
            block = taken[pl.ds(m * n, n), 8 * j:8 * j + 8, :].reshape(n // 2, 2, 8, 128)
            even, odd = swap_rows(block[:, 0], block[:, 1])
            wide[:, 256 * j:256 * j + 128] = even.reshape(4 * n, 128)
            wide[:, 256 * j + 128:256 * j + 256] = odd.reshape(4 * n, 128)
        gram_own[m] = mul_t(wide[...], wide[...])
        swap = pltpu.make_async_remote_copy(
            src_ref=gram_own.at[m], dst_ref=gram_other.at[m], send_sem=gram_send_sem.at[m], recv_sem=gram_sem.at[m],
            device_id={"tp": peer}, device_id_type=MESH)
        swap.start()
        swap.wait()
        factor = -learn_rate * polynomial(gram_own[m] + gram_other[m])
        for j in range(4):
            both = mul(factor, wide[:, 256 * j:256 * j + 256])
            a, b = swap_rows(both[:, :128].reshape(n // 2, 8, 128), both[:, 128:].reshape(n // 2, 8, 128))
            made[pl.ds(m * n, n), 8 * j:8 * j + 8, :] = jnp.stack([a, b], axis=1).reshape(n, 8, 128)
        back[m * n + me] = made[m * n + me]

        def send(to):
            pltpu.make_async_remote_copy(
                src_ref=made.at[m * n + to], dst_ref=back.at[m * n + me], send_sem=send_sem, recv_sem=back_sem.at[m],
                device_id={"fsdp": to}, device_id_type=MESH).start()

        def pair(k, carry):
            send(lax.rem(me + n // 2 - k, n))
            send(lax.rem(me + n // 2 + k, n))
            return carry

        send(lax.rem(me + n // 2, n))
        lax.fori_loop(1, n // 2, pair, 0)
        return carry

    lax.fori_loop(0, chunks, compute, 0)
    for m in range(chunks):
        wait_for(back, back_sem.at[m], m)
    for m in range(2 * chunks):
        wait_for(taken, send_sem, 0)


def body(grad_stack, moment_stack, weight_stack):
    n = lax.axis_size("fsdp")
    mats, rows, cols = grad_stack.shape
    chunks = mats // n

    def tiles(x):
        return x.reshape(mats, rows, cols // 128, 128).transpose(0, 2, 1, 3).reshape(mats, rows * cols // 128, 128)

    def untiles(x):
        return x.reshape(mats, cols // 128, rows, 128).transpose(0, 2, 1, 3).reshape(mats, rows, cols)

    block = (mats, rows * cols // 128, 128)
    side = n * rows
    dma = pltpu.SemaphoreType.DMA
    back, momentum = pl.pallas_call(
        functools.partial(kernel, n, chunks),
        out_shape=[jax.ShapeDtypeStruct(block, F32)] * 2,
        in_specs=[pl.BlockSpec(memory_space=pltpu.HBM)] * 2,
        out_specs=[pl.BlockSpec(memory_space=pltpu.VMEM)] * 2,
        scratch_shapes=[
            pltpu.VMEM(block, F32), pltpu.VMEM(block, F32), pltpu.VMEM(block, F32), pltpu.VMEM(block, F32),
            pltpu.VMEM((side, cols), F32), pltpu.VMEM((chunks, side, side), F32), pltpu.VMEM((chunks, side, side), F32),
            dma((2, chunks)), dma, dma((chunks,)), dma((chunks,)), dma((chunks,)), dma((chunks,)),
        ],
        compiler_params=pltpu.CompilerParams(collective_id=0, has_side_effects=True, vmem_limit_bytes=32 * 2**20),
    )(tiles(grad_stack), tiles(moment_stack))
    new_weights = weight_stack + untiles(back)
    return (new_weights, untiles(momentum))


def solution(mesh):
    spec = P("shift", "fsdp", "tp")
    return jax.shard_map(body, mesh=mesh, in_specs=(spec,) * 3, out_specs=(spec,) * 2, check_vma=False)
```

time: 187 us -> 110 us (0.59)
  Pallas kernels: 0 us -> 103 us
  blocking collectives: 91.4 us -> 0 us
  waiting for transfers between devices: 48.8 us -> 0 us
  matrix products: 18 us -> 0 us
  starting transfers between devices: 11.3 us -> 0 us
  other arithmetic: 8.38 us -> 2.25 us
  local copies, waits for them, and re-layouts: 7.56 us -> 4.5 us
    pallas_call x0 -> x1, Pallas kernels: none -> 103 us  [body(): pl.pallas_call(functools.partial(kernel, n, chunks), out_shape=[jax.Shape...]
    all_to_all x1 -> x0, blocking collectives: 63.8 us -> none  [body(): lax.all_to_all(iterate, 'fsdp', split_axis=1, concat_axis=0, tiled=True)]
    all_to_all x1 -> x0, waiting for transfers between devices: 48.8 us -> none  [body(): lax.all_to_all(new_momentum, 'fsdp', split_axis=0, concat_axis=1, tiled=T...]
    all_gather x3 -> x0, blocking collectives: 22.4 us -> none  [gathered_total(): return lax.all_gather(array, axis).sum(0)]
    dot_general x9 -> x0, matrix products: 18 us -> none  [the longest x3 10.6 us: body(): jnp.einsum('mij,mjk->mik', mixed, iterate, precision=lax.Precision.HIGHEST)]
    all_to_all x1 -> x0, starting transfers between devices: 11.3 us -> none  [body(): lax.all_to_all(new_momentum, 'fsdp', split_axis=0, concat_axis=1, tiled=T...]
    unnamed x1 -> x0, blocking collectives: 5.26 us -> none
    unnamed x11 -> x7, local copies, waits for them, and re-layouts: 0.8 us -> 4.5 us
  transfers between devices with their start and end apart: 1 -> 0, of which waited for: 1 -> 0; matrix products, arithmetic and copies ran while one was open for 0% -> 0% of each run, Pallas kernels for 0% -> 0%
where the time goes in v1:
time: 110 us
  Pallas kernels  103 us (94%)
  local copies, waits for them, and re-layouts  4.5 us (4%)
  other arithmetic  2.25 us (2%)
    pallas_call x1, Pallas kernels, body(): pl.pallas_call(functools.partial(kernel, n, chunks), out_shape=[jax.Shape...  103 us
    unnamed x7, local copies, waits for them, and re-layouts  4.5 us
    add x1, other arithmetic, body(): new_weights = weight_stack + untiles(back)  2.25 us

profile of v1, /device:TPU:1, one launch (start us, length us, event | category | flops | bytes accessed | tf_op | source)
XLA Modules:
  0.0 109.9 jit_solution(11117358089121972139)
XLA Ops:
  0.6 0.0 copy-start
  0.6 1.6 %copy-done = f32[128,4,1024]{2,1,0:T(4,128)S(1)} copy-done((f32[128,4,1024]{2,1,0:T(4,128)S(1)}, f32[128,4,1024]{2,1,0:T(4,128)}, u32[]{:S(2)}) %copy-start) | copy-done | bytes 2097176
  2.2 0.0 copy-start.1
  2.2 1.6 %copy-done.1 = f32[128,4,1024]{2,1,0:T(4,128)S(1)} copy-done((f32[128,4,1024]{2,1,0:T(4,128)S(1)}, f32[128,4,1024]{2,1,0:T(4,128)}, u32[]{:S(2)}) %copy-start.1) | copy-done | bytes 2097176
  3.8 0.0 copy-start.2
  3.8 102.5 %shard_map.50 = (f32[128,32,128]{2,1,0:T(8,128)S(1)}, f32[128,32,128]{2,1,0:T(8,128)S(1)}) custom-call(f32[128,32,128]{2,1,0:T(8,128)S(1)} %bitcast.21, f32[128,32,128]{2,1,0:T(8,128)S(1)} %bitcast.22), custom_call_target="tpu_custom_call" | custom-call | tf_op jit(solution)/shard_map/pallas_call | solution.py:166
  106.4 0.0 copy-done.2
  106.4 2.2 %add.3 = f32[128,4,1024]{2,1,0:T(4,128)} add(f32[128,4,1024]{2,1,0:T(4,128)S(1)} %copy-done.2, f32[128,4,1024]{2,1,0:T(4,128)S(1)} %bitcast.20) | non-fusion elementwise | flops 524288 | bytes 6291456 | tf_op jit(solution)/shard_map/add | solution.py:178
  108.6 1.3 %copy.10 = f32[128,4,1024]{2,1,0:T(4,128)} copy(f32[128,4,1024]{2,1,0:T(4,128)S(1)} %bitcast.23) | data formatting | bytes 4194304
Async XLA Ops:
  0.6 1.6 %copy-start = (f32[128,4,1024]{2,1,0:T(4,128)S(1)}, f32[128,4,1024]{2,1,0:T(4,128)}, u32[]{:S(2)}) copy-start(f32[128,4,1024]{2,1,0:T(4,128)} %param.3) | copy-start | bytes 6291460
  2.2 1.6 %copy-start.1 = (f32[128,4,1024]{2,1,0:T(4,128)S(1)}, f32[128,4,1024]{2,1,0:T(4,128)}, u32[]{:S(2)}) copy-start(f32[128,4,1024]{2,1,0:T(4,128)} %param.4) | copy-start | bytes 6291460
  3.8 102.5 %copy-start.2 = (f32[128,4,1024]{2,1,0:T(4,128)S(1)}, f32[128,4,1024]{2,1,0:T(4,128)}, u32[]{:S(2)}) copy-start(f32[128,4,1024]{2,1,0:T(4,128)} %param.5) | copy-start | bytes 6291460

commit v2 on v1

--- a/solution.py
+++ b/solution.py
@@ -8,6 +8,7 @@
 from jax.sharding import PartitionSpec as P
 
 ITERS = 3
+GROUPS = 8
 hold_rate = 0.95
 learn_rate = 0.9
 
@@ -50,7 +51,8 @@
 
 
 def kernel(n, chunks, grad_hbm, moment_hbm, back, mom, grads, moments, taken, made, wide, gram_own, gram_other,
-           load_sem, send_sem, in_sem, gram_send_sem, gram_sem, back_sem):
+           load_sem, send_sem, in_sem, gram_send_sem, gram_sem, back_sem,
+           round_sem):
     me = lax.axis_index("fsdp")
     tp = lax.axis_index("tp")
     peer = 1 - tp
@@ -66,13 +68,16 @@
         for copy in loads(m):
             copy.start()
 
+    group = n // GROUPS
+    z, q = me // group, me % group
+
+    def at(dz, dq):
+        return lax.rem(z + dz, GROUPS) * group + lax.rem(q + dq, group)
+
     barrier = pltpu.get_barrier_semaphore()
-
-    def greet(k, carry):
-        pl.semaphore_signal(barrier, inc=1, device_id={"fsdp": lax.rem(me + k, n)}, device_id_type=MESH)
-        return carry
-
-    lax.fori_loop(1, n, greet, 0)
+    for dq in range(group):
+        for dz in (1, GROUPS - 1) + ((0,) if dq else ()):
+            pl.semaphore_signal(barrier, inc=1, device_id={"fsdp": at(dz, dq)}, device_id_type=MESH)
     pl.semaphore_signal(barrier, inc=1, device_id={"tp": peer}, device_id_type=MESH)
 
     def momentum(m):
@@ -82,27 +87,37 @@
         mom[rows] = hold_rate * moments[rows] + grads[rows]
         taken[m * n + me] = mom[m * n + me]
 
+    def sender(source, target, sem, m):
+        def send(dz, dq):
+            to = at(dz, dq)
+            pltpu.make_async_remote_copy(
+                src_ref=source.at[m * n + to], dst_ref=target.at[m * n + me], send_sem=send_sem, recv_sem=sem.at[m],
+                device_id={"fsdp": to}, device_id_type=MESH).start()
+
+        def sends(distances, first=0):
+            def at_index(dq, carry):
+                for dz in distances:
+                    send(dz, dq)
+                return carry
+
+            lax.fori_loop(first, group, at_index, 0)
+
+        return sends
+
     momentum(0)
-    pl.semaphore_wait(barrier, n)
-
-    def scatter(m):
-        def send(to):
-            pltpu.make_async_remote_copy(
-                src_ref=mom.at[m * n + to], dst_ref=taken.at[m * n + me], send_sem=send_sem, recv_sem=in_sem.at[m],
-                device_id={"fsdp": to}, device_id_type=MESH).start()
-
-        def pair(k, carry):
-            send(lax.rem(me + n // 2 - k, n))
-            send(lax.rem(me + n // 2 + k, n))
-            return carry
-
-        send(lax.rem(me + n // 2, n))
-        lax.fori_loop(1, n // 2, pair, 0)
-
+    pl.semaphore_wait(barrier, 3 * group)
     for m in range(chunks):
         if m:
             momentum(m)
-        scatter(m)
+        sends = sender(mom, taken, in_sem, m)
+        sends((1, GROUPS - 1))
+        sends((0,), 1)
+    for step in range(3):
+        for dz in (1, GROUPS - 1):
+            pl.semaphore_signal(round_sem.at[step], inc=1, device_id={"fsdp": at(dz, 0)}, device_id_type=MESH)
+        pl.semaphore_wait(round_sem.at[step], 2)
+    for m in range(chunks):
+        sender(mom, taken, in_sem, m)((3, 5, 4, 2, 6))
 
     def wait_for(buffer, sem, m):
         part = buffer.at[pl.ds(m * n, n - 1)]
@@ -128,18 +143,9 @@
             made[pl.ds(m * n, n), 8 * j:8 * j + 8, :] = jnp.stack([a, b], axis=1).reshape(n, 8, 128)
         back[m * n + me] = made[m * n + me]
 
-        def send(to):
-            pltpu.make_async_remote_copy(
-                src_ref=made.at[m * n + to], dst_ref=back.at[m * n + me], send_sem=send_sem, recv_sem=back_sem.at[m],
-                device_id={"fsdp": to}, device_id_type=MESH).start()
-
-        def pair(k, carry):
-            send(lax.rem(me + n // 2 - k, n))
-            send(lax.rem(me + n // 2 + k, n))
-            return carry
-
-        send(lax.rem(me + n // 2, n))
-        lax.fori_loop(1, n // 2, pair, 0)
+        sends = sender(made, back, back_sem, m)
+        sends((3, 5, 4, 2, 6, 1, 7))
+        sends((0,), 1)
         return carry
 
     lax.fori_loop(0, chunks, compute, 0)
@@ -147,6 +153,19 @@
         wait_for(back, back_sem.at[m], m)
     for m in range(2 * chunks):
         wait_for(taken, send_sem, 0)
+
+
+def finish(parts, weight, back, mom, weight_out, mom_out, total, sem):
+    copies = [pltpu.make_async_copy(mom, mom_out, sem.at[parts])]
+    copies[0].start()
+    size = weight.shape[0] // parts
+    for i in range(parts):
+        rows = pl.ds(i * size, size)
+        total[rows] = weight[rows] + back[rows]
+        copies.append(pltpu.make_async_copy(total.at[rows], weight_out.at[rows], sem.at[i]))
+        copies[-1].start()
+    for copy in copies:
+        copy.wait()
 
 
 def body(grad_stack, moment_stack, weight_stack):
@@ -172,11 +191,19 @@
             pltpu.VMEM(block, F32), pltpu.VMEM(block, F32), pltpu.VMEM(block, F32), pltpu.VMEM(block, F32),
             pltpu.VMEM((side, cols), F32), pltpu.VMEM((chunks, side, side), F32), pltpu.VMEM((chunks, side, side), F32),
             dma((2, chunks)), dma, dma((chunks,)), dma((chunks,)), dma((chunks,)), dma((chunks,)),
+            pltpu.SemaphoreType.REGULAR((3,)),
         ],
         compiler_params=pltpu.CompilerParams(collective_id=0, has_side_effects=True, vmem_limit_bytes=32 * 2**20),
-    )(tiles(grad_stack), tiles(moment_stack))
-    new_weights = weight_stack + untiles(back)
-    return (new_weights, untiles(momentum))
+    )(*(pltpu.with_memory_space_constraint(tiles(x), pltpu.HBM) for x in (grad_stack, moment_stack)))
+    new_weights, new_momentum = pl.pallas_call(
+        functools.partial(finish, 4),
+        out_shape=[jax.ShapeDtypeStruct(block, F32)] * 2,
+        in_specs=[pl.BlockSpec(memory_space=pltpu.VMEM)] * 3,
+        out_specs=[pl.BlockSpec(memory_space=pl.ANY)] * 2,
+        scratch_shapes=[pltpu.VMEM(block, F32), dma((5,))],
+        compiler_params=pltpu.CompilerParams(vmem_limit_bytes=8 * 2**20),
+    )(tiles(weight_stack), back, momentum)
+    return (untiles(new_weights), untiles(new_momentum))
 
 
 def solution(mesh):

time: 110 us -> 104 us (0.945)
  local copies, waits for them, and re-layouts: 4.5 us -> 0.01 us
  other arithmetic: 2.25 us -> 0 us
    unnamed x7 -> x2, local copies, waits for them, and re-layouts: 4.5 us -> 0.01 us
    add x1 -> x0, other arithmetic: 2.25 us -> none  [body(): new_weights = weight_stack + untiles(back)]
    pallas_call x0 -> x1, Pallas kernels: none -> 2.05 us  [body(): pl.pallas_call(functools.partial(finish, 4), out_shape=[jax.ShapeDtypeStr...]
    pallas_call x1, Pallas kernels: 103 us -> 101 us  [body(): pl.pallas_call(functools.partial(kernel, n, chunks), out_shape=[jax.Shape...]
where the time goes in v2:
time: 104 us
  Pallas kernels  103 us (99%)
    pallas_call x1, Pallas kernels, body(): pl.pallas_call(functools.partial(kernel, n, chunks), out_shape=[jax.Shape...  101 us

profile of v2, /device:TPU:1, one launch (start us, length us, event | category | flops | bytes accessed | tf_op | source)
XLA Modules:
  0.0 103.5 jit_solution(16268843878859413976)
XLA Ops:
  0.6 0.0 copy-start
  0.6 100.8 %shard_map.50 = (f32[128,32,128]{2,1,0:T(8,128)S(1)}, f32[128,32,128]{2,1,0:T(8,128)S(1)}) custom-call(f32[128,32,128]{2,1,0:T(8,128)} %bitcast.26, f32[128,32,128]{2,1,0:T(8,128)} %bitcast.27), custom_call_target="tpu_custom_call" | custom-call | tf_op jit(solution)/shard_map/pallas_call | solution.py:185
  101.5 0.0 copy-done
  101.5 2.0 %shard_map.51 = (f32[128,32,128]{2,1,0:T(8,128)}, f32[128,32,128]{2,1,0:T(8,128)}) custom-call(f32[128,32,128]{2,1,0:T(8,128)S(1)} %bitcast.25, f32[128,32,128]{2,1,0:T(8,128)S(1)} %get-tuple-element.6.back, f32[128,32,128]{2,1,0:T(8,128)S(1)} %get-tuple-element.7.mom), custom_call_target="tpu_custom_call" | custom-call | tf_op jit(solution)/shard_map/pallas_call | solution.py:198
Async XLA Ops:
  0.6 100.8 %copy-start = (f32[128,4,1024]{2,1,0:T(4,128)S(1)}, f32[128,4,1024]{2,1,0:T(4,128)}, u32[]{:S(2)}) copy-start(f32[128,4,1024]{2,1,0:T(4,128)} %param.5) | copy-start | bytes 6291460

commit v3 on v2

--- a/solution.py
+++ b/solution.py
@@ -8,13 +8,27 @@
 from jax.sharding import PartitionSpec as P
 
 ITERS = 3
-GROUPS = 8
+DEPTH = 8
+GROUP = 4
 hold_rate = 0.95
 learn_rate = 0.9
 
 MESH = pl.DeviceIdType.MESH
 HIGHEST = lax.Precision.HIGHEST
 F32 = jnp.float32
+
+
+OWN, BESIDE, ACROSS, OBLIQUE, FIRST, SECOND, THIRD, FOURTH = range(8)
+ROW, NEXT, TURNS = (OWN, BESIDE), (ACROSS, OBLIQUE), (FIRST, SECOND, THIRD, FOURTH)
+ZERO = ((0, BESIDE), (0, ACROSS), (0, OBLIQUE))
+
+
+def moves(distances, places):
+    return tuple((dz, place) for place in places for dz in distances)
+
+
+OUT = ZERO + moves((4,), TURNS) + moves((3, 5), TURNS) + moves((2, 6), TURNS) + moves((1, 7), TURNS)
+LAST = ((0, 4), (4, 8), (8, 32))
 
 
 def mul(a, b):
@@ -68,16 +82,18 @@
         for copy in loads(m):
             copy.start()
 
-    group = n // GROUPS
-    z, q = me // group, me % group
-
-    def at(dz, dq):
-        return lax.rem(z + dz, GROUPS) * group + lax.rem(q + dq, group)
+    z, q = me // GROUP, me % GROUP
+    odd = q % 2
+    places = {OWN: 0, BESIDE: 1 + 2 * odd, ACROSS: 2, OBLIQUE: 3 - 2 * odd,
+              FIRST: 2 * odd, SECOND: 2 - 2 * odd, THIRD: 1, FOURTH: 3}
+
+    def at(dz, place):
+        return lax.rem(z + dz, DEPTH) * GROUP + lax.rem(q + places[place], GROUP)
 
     barrier = pltpu.get_barrier_semaphore()
-    for dq in range(group):
-        for dz in (1, GROUPS - 1) + ((0,) if dq else ()):
-            pl.semaphore_signal(barrier, inc=1, device_id={"fsdp": at(dz, dq)}, device_id_type=MESH)
+    greeted = moves((1, DEPTH - 1), TURNS) + ZERO
+    for shift in greeted:
+        pl.semaphore_signal(barrier, inc=1, device_id={"fsdp": at(*shift)}, device_id_type=MESH)
     pl.semaphore_signal(barrier, inc=1, device_id={"tp": peer}, device_id_type=MESH)
 
     def momentum(m):
@@ -87,38 +103,46 @@
         mom[rows] = hold_rate * moments[rows] + grads[rows]
         taken[m * n + me] = mom[m * n + me]
 
-    def sender(source, target, sem, m):
-        def send(dz, dq):
-            to = at(dz, dq)
+    def send(source, target, sem, m, to_shifts):
+        for shift in to_shifts:
+            to = at(*shift)
             pltpu.make_async_remote_copy(
                 src_ref=source.at[m * n + to], dst_ref=target.at[m * n + me], send_sem=send_sem, recv_sem=sem.at[m],
                 device_id={"fsdp": to}, device_id_type=MESH).start()
 
-        def sends(distances, first=0):
-            def at_index(dq, carry):
-                for dz in distances:
-                    send(dz, dq)
-                return carry
-
-            lax.fori_loop(first, group, at_index, 0)
-
-        return sends
+    def send_some(source, target, sem, m, to_moves, low, high):
+        for move in to_moves:
+            to = at(*move)
+
+            @pl.when((to >= low) & (to < high))
+            def _():
+                pltpu.make_async_remote_copy(
+                    src_ref=source.at[m * n + to], dst_ref=target.at[m * n + me], send_sem=send_sem,
+                    recv_sem=sem.at[m], device_id={"fsdp": to}, device_id_type=MESH).start()
+
+    def scatter(first, last, to_shifts):
+        def one(m, carry):
+            send(mom, taken, in_sem, m, to_shifts)
+            return carry
+
+        lax.fori_loop(first, last, one, 0)
+
+    def round_of(step):
+        for dz in (1, DEPTH - 1):
+            pl.semaphore_signal(round_sem.at[step], inc=1, device_id={"fsdp": at(dz, OWN)}, device_id_type=MESH)
+        pl.semaphore_wait(round_sem.at[step], 2)
 
     momentum(0)
-    pl.semaphore_wait(barrier, 3 * group)
+    pl.semaphore_wait(barrier, len(greeted) + 1)
     for m in range(chunks):
         if m:
             momentum(m)
-        sends = sender(mom, taken, in_sem, m)
-        sends((1, GROUPS - 1))
-        sends((0,), 1)
-    for step in range(3):
-        for dz in (1, GROUPS - 1):
-            pl.semaphore_signal(round_sem.at[step], inc=1, device_id={"fsdp": at(dz, 0)}, device_id_type=MESH)
-        pl.semaphore_wait(round_sem.at[step], 2)
-    for m in range(chunks):
-        sender(mom, taken, in_sem, m)((3, 5, 4, 2, 6))
-
+        send(mom, taken, in_sem, m, moves((1, 7), ROW) + ZERO)
+    round_of(0)
+    scatter(0, chunks, moves((2, 6), ROW))
+    round_of(1)
+    round_of(2)
+    scatter(0, chunks, moves((4, 3, 5), TURNS) + moves((2, 6, 1, 7), NEXT))
     def wait_for(buffer, sem, m):
         part = buffer.at[pl.ds(m * n, n - 1)]
         pltpu.make_async_copy(part, part, sem).wait()
@@ -143,9 +167,15 @@
             made[pl.ds(m * n, n), 8 * j:8 * j + 8, :] = jnp.stack([a, b], axis=1).reshape(n, 8, 128)
         back[m * n + me] = made[m * n + me]
 
-        sends = sender(made, back, back_sem, m)
-        sends((3, 5, 4, 2, 6, 1, 7))
-        sends((0,), 1)
+        @pl.when(m < chunks - 1)
+        def _():
+            send(made, back, back_sem, m, OUT)
+
+        @pl.when(m == chunks - 1)
+        def _():
+            for low, high in LAST:
+                send_some(made, back, back_sem, m, OUT, low, high)
+
         return carry
 
     lax.fori_loop(0, chunks, compute, 0)

time: 104 us -> 102 us (0.981)
  Pallas kernels: 103 us -> 100 us
    pallas_call x1, Pallas kernels: 101 us -> 98.4 us  [body(): pl.pallas_call(functools.partial(kernel, n, chunks), out_shape=[jax.Shape...]
where the time goes in v3:
time: 102 us; the launch traced here: 101 us
  Pallas kernels  100 us (98%)
    pallas_call x1, Pallas kernels, body(): pl.pallas_call(functools.partial(kernel, n, chunks), out_shape=[jax.Shape...  98.4 us
    pallas_call x1, Pallas kernels, body(): pl.pallas_call(functools.partial(finish, 4), out_shape=[jax.ShapeDtypeStr...  2.05 us

profile of v3, /device:TPU:1, one launch (start us, length us, event | category | flops | bytes accessed | tf_op | source)
XLA Modules:
  0.0 101.1 jit_solution(5117419022278154151)
XLA Ops:
  0.6 0.0 copy-start
  0.6 98.4 %shard_map.50 = (f32[128,32,128]{2,1,0:T(8,128)S(1)}, f32[128,32,128]{2,1,0:T(8,128)S(1)}) custom-call(f32[128,32,128]{2,1,0:T(8,128)} %bitcast.26, f32[128,32,128]{2,1,0:T(8,128)} %bitcast.27), custom_call_target="tpu_custom_call" | custom-call | tf_op jit(solution)/shard_map/pallas_call | solution.py:215
  99.0 0.0 copy-done
  99.0 2.0 %shard_map.51 = (f32[128,32,128]{2,1,0:T(8,128)}, f32[128,32,128]{2,1,0:T(8,128)}) custom-call(f32[128,32,128]{2,1,0:T(8,128)S(1)} %bitcast.25, f32[128,32,128]{2,1,0:T(8,128)S(1)} %get-tuple-element.6.back, f32[128,32,128]{2,1,0:T(8,128)S(1)} %get-tuple-element.7.mom), custom_call_target="tpu_custom_call" | custom-call | tf_op jit(solution)/shard_map/pallas_call | solution.py:228
Async XLA Ops:
  0.6 98.4 %copy-start = (f32[128,4,1024]{2,1,0:T(4,128)S(1)}, f32[128,4,1024]{2,1,0:T(4,128)}, u32[]{:S(2)}) copy-start(f32[128,4,1024]{2,1,0:T(4,128)} %param.5) | copy-start | bytes 6291460

commit v4 on v3

--- a/solution.py
+++ b/solution.py
@@ -27,7 +27,7 @@
     return tuple((dz, place) for place in places for dz in distances)
 
 
-OUT = ZERO + moves((4,), TURNS) + moves((3, 5), TURNS) + moves((2, 6), TURNS) + moves((1, 7), TURNS)
+OUT = ZERO + moves((4,), TURNS) + moves((5, 3), TURNS) + moves((6, 2), TURNS) + moves((7, 1), TURNS)
 LAST = ((0, 4), (4, 8), (8, 32))
 
 

time: 102 us -> 102 us (level)
  no operation moved by 1% of the time
where the time goes in v4:
time: 102 us; the launch traced here: 101 us
  Pallas kernels  100 us (98%)
    pallas_call x1, Pallas kernels, body(): pl.pallas_call(functools.partial(kernel, n, chunks), out_shape=[jax.Shape...  98.4 us
    pallas_call x1, Pallas kernels, body(): pl.pallas_call(functools.partial(finish, 4), out_shape=[jax.ShapeDtypeStr...  2.05 us

profile of v4, /device:TPU:1, one launch (start us, length us, event | category | flops | bytes accessed | tf_op | source)
XLA Modules:
  0.0 101.1 jit_solution(18242635241931125293)
XLA Ops:
  0.6 0.0 copy-start
  0.6 98.4 %shard_map.50 = (f32[128,32,128]{2,1,0:T(8,128)S(1)}, f32[128,32,128]{2,1,0:T(8,128)S(1)}) custom-call(f32[128,32,128]{2,1,0:T(8,128)} %bitcast.26, f32[128,32,128]{2,1,0:T(8,128)} %bitcast.27), custom_call_target="tpu_custom_call" | custom-call | tf_op jit(solution)/shard_map/pallas_call | solution.py:215
  99.0 0.0 copy-done
  99.0 2.0 %shard_map.51 = (f32[128,32,128]{2,1,0:T(8,128)}, f32[128,32,128]{2,1,0:T(8,128)}) custom-call(f32[128,32,128]{2,1,0:T(8,128)S(1)} %bitcast.25, f32[128,32,128]{2,1,0:T(8,128)S(1)} %get-tuple-element.6.back, f32[128,32,128]{2,1,0:T(8,128)S(1)} %get-tuple-element.7.mom), custom_call_target="tpu_custom_call" | custom-call | tf_op jit(solution)/shard_map/pallas_call | solution.py:228
Async XLA Ops:
  0.6 98.4 %copy-start = (f32[128,4,1024]{2,1,0:T(4,128)S(1)}, f32[128,4,1024]{2,1,0:T(4,128)}, u32[]{:S(2)}) copy-start(f32[128,4,1024]{2,1,0:T(4,128)} %param.5) | copy-start | bytes 6291460

commit v5 on v4

--- a/solution.py
+++ b/solution.py
@@ -91,7 +91,7 @@
         return lax.rem(z + dz, DEPTH) * GROUP + lax.rem(q + places[place], GROUP)
 
     barrier = pltpu.get_barrier_semaphore()
-    greeted = moves((1, DEPTH - 1), TURNS) + ZERO
+    greeted = moves((1, DEPTH - 1), ROW) + ((0, BESIDE), (0, ACROSS))
     for shift in greeted:
         pl.semaphore_signal(barrier, inc=1, device_id={"fsdp": at(*shift)}, device_id_type=MESH)
     pl.semaphore_signal(barrier, inc=1, device_id={"tp": peer}, device_id_type=MESH)
@@ -128,20 +128,22 @@
         lax.fori_loop(first, last, one, 0)
 
     def round_of(step):
-        for dz in (1, DEPTH - 1):
-            pl.semaphore_signal(round_sem.at[step], inc=1, device_id={"fsdp": at(dz, OWN)}, device_id_type=MESH)
-        pl.semaphore_wait(round_sem.at[step], 2)
+        told = ((1, OWN), (DEPTH - 1, OWN)) + (((0, ACROSS),) if step == 0 else ())
+        for move in told:
+            pl.semaphore_signal(round_sem.at[step], inc=1, device_id={"fsdp": at(*move)}, device_id_type=MESH)
+        pl.semaphore_wait(round_sem.at[step], len(told))
 
     momentum(0)
     pl.semaphore_wait(barrier, len(greeted) + 1)
     for m in range(chunks):
         if m:
             momentum(m)
-        send(mom, taken, in_sem, m, moves((1, 7), ROW) + ZERO)
+        send(mom, taken, in_sem, m, moves((1, 7), ROW) + ((0, BESIDE), (0, ACROSS)))
     round_of(0)
-    scatter(0, chunks, moves((2, 6), ROW))
+    scatter(0, chunks, moves((2, 6), ROW) + ((0, OBLIQUE),))
     round_of(1)
     round_of(2)
+    round_of(3)
     scatter(0, chunks, moves((4, 3, 5), TURNS) + moves((2, 6, 1, 7), NEXT))
     def wait_for(buffer, sem, m):
         part = buffer.at[pl.ds(m * n, n - 1)]
@@ -221,7 +223,7 @@
             pltpu.VMEM(block, F32), pltpu.VMEM(block, F32), pltpu.VMEM(block, F32), pltpu.VMEM(block, F32),
             pltpu.VMEM((side, cols), F32), pltpu.VMEM((chunks, side, side), F32), pltpu.VMEM((chunks, side, side), F32),
             dma((2, chunks)), dma, dma((chunks,)), dma((chunks,)), dma((chunks,)), dma((chunks,)),
-            pltpu.SemaphoreType.REGULAR((3,)),
+            pltpu.SemaphoreType.REGULAR((4,)),
         ],
         compiler_params=pltpu.CompilerParams(collective_id=0, has_side_effects=True, vmem_limit_bytes=32 * 2**20),
     )(*(pltpu.with_memory_space_constraint(tiles(x), pltpu.HBM) for x in (grad_stack, moment_stack)))

time: 102 us -> 102 us (level)
  no operation moved by 1% of the time
where the time goes in v5:
time: 102 us; the launch traced here: 101 us
  Pallas kernels  101 us (99%)
    pallas_call x1, Pallas kernels, body(): pl.pallas_call(functools.partial(kernel, n, chunks), out_shape=[jax.Shape...  98.8 us
    pallas_call x1, Pallas kernels, body(): pl.pallas_call(functools.partial(finish, 4), out_shape=[jax.ShapeDtypeStr...  2.05 us

profile of v5, /device:TPU:1, one launch (start us, length us, event | category | flops | bytes accessed | tf_op | source)
XLA Modules:
  0.0 101.5 jit_solution(7754863277671748507)
XLA Ops:
  0.6 0.0 copy-start
  0.6 98.8 %shard_map.50 = (f32[128,32,128]{2,1,0:T(8,128)S(1)}, f32[128,32,128]{2,1,0:T(8,128)S(1)}) custom-call(f32[128,32,128]{2,1,0:T(8,128)} %bitcast.26, f32[128,32,128]{2,1,0:T(8,128)} %bitcast.27), custom_call_target="tpu_custom_call" | custom-call | tf_op jit(solution)/shard_map/pallas_call | solution.py:217
  99.4 0.0 copy-done
  99.4 2.0 %shard_map.51 = (f32[128,32,128]{2,1,0:T(8,128)}, f32[128,32,128]{2,1,0:T(8,128)}) custom-call(f32[128,32,128]{2,1,0:T(8,128)S(1)} %bitcast.25, f32[128,32,128]{2,1,0:T(8,128)S(1)} %get-tuple-element.6.back, f32[128,32,128]{2,1,0:T(8,128)S(1)} %get-tuple-element.7.mom), custom_call_target="tpu_custom_call" | custom-call | tf_op jit(solution)/shard_map/pallas_call | solution.py:230
Async XLA Ops:
  0.6 98.8 %copy-start = (f32[128,4,1024]{2,1,0:T(4,128)S(1)}, f32[128,4,1024]{2,1,0:T(4,128)}, u32[]{:S(2)}) copy-start(f32[128,4,1024]{2,1,0:T(4,128)} %param.5) | copy-start | bytes 6291460

commit v6 on v5

--- a/solution.py
+++ b/solution.py
@@ -64,7 +64,7 @@
     return factor * scale
 
 
-def kernel(n, chunks, grad_hbm, moment_hbm, back, mom, grads, moments, taken, made, wide, gram_own, gram_other,
+def kernel(n, chunks, grad_hbm, moment_hbm, weight_hbm, back, mom, weights, weight_sem, grads, moments, taken, made, wide, gram_own, gram_other,
            load_sem, send_sem, in_sem, gram_send_sem, gram_sem, back_sem,
            round_sem):
     me = lax.axis_index("fsdp")
@@ -180,22 +180,22 @@
 
         return carry
 
+    weight_load = pltpu.make_async_copy(weight_hbm, weights, weight_sem)
+    weight_load.start()
     lax.fori_loop(0, chunks, compute, 0)
+    weight_load.wait()
     for m in range(chunks):
         wait_for(back, back_sem.at[m], m)
+        rows = pl.ds(m * n, n)
+        back[rows] = weights[rows] + back[rows]
     for m in range(2 * chunks):
         wait_for(taken, send_sem, 0)
 
 
-def finish(parts, weight, back, mom, weight_out, mom_out, total, sem):
-    copies = [pltpu.make_async_copy(mom, mom_out, sem.at[parts])]
-    copies[0].start()
-    size = weight.shape[0] // parts
-    for i in range(parts):
-        rows = pl.ds(i * size, size)
-        total[rows] = weight[rows] + back[rows]
-        copies.append(pltpu.make_async_copy(total.at[rows], weight_out.at[rows], sem.at[i]))
-        copies[-1].start()
+def finish(weight, mom, weight_out, mom_out, sem):
+    copies = (pltpu.make_async_copy(weight, weight_out, sem.at[0]), pltpu.make_async_copy(mom, mom_out, sem.at[1]))
+    for copy in copies:
+        copy.start()
     for copy in copies:
         copy.wait()
 
@@ -217,24 +217,25 @@
     back, momentum = pl.pallas_call(
         functools.partial(kernel, n, chunks),
         out_shape=[jax.ShapeDtypeStruct(block, F32)] * 2,
-        in_specs=[pl.BlockSpec(memory_space=pltpu.HBM)] * 2,
+        in_specs=[pl.BlockSpec(memory_space=pltpu.HBM)] * 3,
         out_specs=[pl.BlockSpec(memory_space=pltpu.VMEM)] * 2,
         scratch_shapes=[
+            pltpu.VMEM(block, F32), dma,
             pltpu.VMEM(block, F32), pltpu.VMEM(block, F32), pltpu.VMEM(block, F32), pltpu.VMEM(block, F32),
             pltpu.VMEM((side, cols), F32), pltpu.VMEM((chunks, side, side), F32), pltpu.VMEM((chunks, side, side), F32),
             dma((2, chunks)), dma, dma((chunks,)), dma((chunks,)), dma((chunks,)), dma((chunks,)),
             pltpu.SemaphoreType.REGULAR((4,)),
         ],
         compiler_params=pltpu.CompilerParams(collective_id=0, has_side_effects=True, vmem_limit_bytes=32 * 2**20),
-    )(*(pltpu.with_memory_space_constraint(tiles(x), pltpu.HBM) for x in (grad_stack, moment_stack)))
+    )(*(pltpu.with_memory_space_constraint(tiles(x), pltpu.HBM) for x in (grad_stack, moment_stack, weight_stack)))
     new_weights, new_momentum = pl.pallas_call(
-        functools.partial(finish, 4),
+        finish,
         out_shape=[jax.ShapeDtypeStruct(block, F32)] * 2,
-        in_specs=[pl.BlockSpec(memory_space=pltpu.VMEM)] * 3,
+        in_specs=[pl.BlockSpec(memory_space=pltpu.VMEM)] * 2,
         out_specs=[pl.BlockSpec(memory_space=pl.ANY)] * 2,
-        scratch_shapes=[pltpu.VMEM(block, F32), dma((5,))],
+        scratch_shapes=[dma((2,))],
         compiler_params=pltpu.CompilerParams(vmem_limit_bytes=8 * 2**20),
-    )(tiles(weight_stack), back, momentum)
+    )(back, momentum)
     return (untiles(new_weights), untiles(new_momentum))
 
 

time: 102 us -> 102 us (level)
  no operation moved by 1% of the time
where the time goes in v6:
time: 102 us
  Pallas kernels  102 us (100%)
    pallas_call x1, Pallas kernels, body(): pl.pallas_call(functools.partial(kernel, n, chunks), out_shape=[jax.Shape...  99.5 us

profile of v6, /device:TPU:1, one launch (start us, length us, event | category | flops | bytes accessed | tf_op | source)
XLA Modules:
  0.0 102.2 jit_solution(3854653175071625110)
XLA Ops:
  0.6 99.5 %shard_map.50 = (f32[128,32,128]{2,1,0:T(8,128)S(1)}, f32[128,32,128]{2,1,0:T(8,128)S(1)}) custom-call(f32[128,32,128]{2,1,0:T(8,128)} %bitcast.25, f32[128,32,128]{2,1,0:T(8,128)} %bitcast.26, f32[128,32,128]{2,1,0:T(8,128)} %bitcast.27), custom_call_target="tpu_custom_call" | custom-call | tf_op jit(solution)/shard_map/pallas_call | solution.py:217
  100.1 2.0 %shard_map.51 = (f32[128,32,128]{2,1,0:T(8,128)}, f32[128,32,128]{2,1,0:T(8,128)}) custom-call(f32[128,32,128]{2,1,0:T(8,128)S(1)} %get-tuple-element.6.weight, f32[128,32,128]{2,1,0:T(8,128)S(1)} %get-tuple-element.7.mom), custom_call_target="tpu_custom_call" | custom-call | tf_op jit(solution)/shard_map/pallas_call | solution.py:231

commit v7 on v5

--- a/solution.py
+++ b/solution.py
@@ -27,7 +27,7 @@
     return tuple((dz, place) for place in places for dz in distances)
 
 
-OUT = ZERO + moves((4,), TURNS) + moves((5, 3), TURNS) + moves((6, 2), TURNS) + moves((7, 1), TURNS)
+OUT = moves((4,), TURNS) + moves((5, 3), TURNS) + moves((6, 2), TURNS) + moves((7, 1), TURNS) + ZERO
 LAST = ((0, 4), (4, 8), (8, 32))
 
 

time: 102 us -> 102 us (level)
  no operation moved by 1% of the time
where the time goes in v7:
time: 102 us
  Pallas kernels  102 us (100%)
    pallas_call x1, Pallas kernels, body(): pl.pallas_call(functools.partial(kernel, n, chunks), out_shape=[jax.Shape...  99.5 us
    pallas_call x1, Pallas kernels, body(): pl.pallas_call(functools.partial(finish, 4), out_shape=[jax.ShapeDtypeStr...  2.05 us

profile of v7, /device:TPU:1, one launch (start us, length us, event | category | flops | bytes accessed | tf_op | source)
XLA Modules:
  0.0 102.2 jit_solution(6616586380181437407)
XLA Ops:
  0.6 0.0 copy-start
  0.6 99.5 %shard_map.50 = (f32[128,32,128]{2,1,0:T(8,128)S(1)}, f32[128,32,128]{2,1,0:T(8,128)S(1)}) custom-call(f32[128,32,128]{2,1,0:T(8,128)} %bitcast.26, f32[128,32,128]{2,1,0:T(8,128)} %bitcast.27), custom_call_target="tpu_custom_call" | custom-call | tf_op jit(solution)/shard_map/pallas_call | solution.py:217
  100.1 0.0 copy-done
  100.1 2.0 %shard_map.51 = (f32[128,32,128]{2,1,0:T(8,128)}, f32[128,32,128]{2,1,0:T(8,128)}) custom-call(f32[128,32,128]{2,1,0:T(8,128)S(1)} %bitcast.25, f32[128,32,128]{2,1,0:T(8,128)S(1)} %get-tuple-element.6.back, f32[128,32,128]{2,1,0:T(8,128)S(1)} %get-tuple-element.7.mom), custom_call_target="tpu_custom_call" | custom-call | tf_op jit(solution)/shard_map/pallas_call | solution.py:230
Async XLA Ops:
  0.6 99.5 %copy-start = (f32[128,4,1024]{2,1,0:T(4,128)S(1)}, f32[128,4,1024]{2,1,0:T(4,128)}, u32[]{:S(2)}) copy-start(f32[128,4,1024]{2,1,0:T(4,128)} %param.5) | copy-start | bytes 6291460

commit v8 on v5

--- a/solution.py
+++ b/solution.py
@@ -28,7 +28,7 @@
 
 
 OUT = ZERO + moves((4,), TURNS) + moves((5, 3), TURNS) + moves((6, 2), TURNS) + moves((7, 1), TURNS)
-LAST = ((0, 4), (4, 8), (8, 32))
+LAST = ((0, 4), (4, 8), (8, 10), (10, 32))
 
 
 def mul(a, b):

time: 102 us -> 102 us (level)
  no operation moved by 1% of the time
where the time goes in v8:
time: 102 us; the launch traced here: 101 us
  Pallas kernels  101 us (99%)
    pallas_call x1, Pallas kernels, body(): pl.pallas_call(functools.partial(kernel, n, chunks), out_shape=[jax.Shape...  98.6 us
    pallas_call x1, Pallas kernels, body(): pl.pallas_call(functools.partial(finish, 4), out_shape=[jax.ShapeDtypeStr...  2.05 us

profile of v8, /device:TPU:1, one launch (start us, length us, event | category | flops | bytes accessed | tf_op | source)
XLA Modules:
  0.0 101.3 jit_solution(6461190309081917599)
XLA Ops:
  0.6 0.0 copy-start
  0.6 98.6 %shard_map.50 = (f32[128,32,128]{2,1,0:T(8,128)S(1)}, f32[128,32,128]{2,1,0:T(8,128)S(1)}) custom-call(f32[128,32,128]{2,1,0:T(8,128)} %bitcast.26, f32[128,32,128]{2,1,0:T(8,128)} %bitcast.27), custom_call_target="tpu_custom_call" | custom-call | tf_op jit(solution)/shard_map/pallas_call | solution.py:217
  99.3 0.0 copy-done
  99.3 2.0 %shard_map.51 = (f32[128,32,128]{2,1,0:T(8,128)}, f32[128,32,128]{2,1,0:T(8,128)}) custom-call(f32[128,32,128]{2,1,0:T(8,128)S(1)} %bitcast.25, f32[128,32,128]{2,1,0:T(8,128)S(1)} %get-tuple-element.6.back, f32[128,32,128]{2,1,0:T(8,128)S(1)} %get-tuple-element.7.mom), custom_call_target="tpu_custom_call" | custom-call | tf_op jit(solution)/shard_map/pallas_call | solution.py:230
Async XLA Ops:
  0.6 98.7 %copy-start = (f32[128,4,1024]{2,1,0:T(4,128)S(1)}, f32[128,4,1024]{2,1,0:T(4,128)}, u32[]{:S(2)}) copy-start(f32[128,4,1024]{2,1,0:T(4,128)} %param.5) | copy-start | bytes 6291460
